TPU v7x, 32 devices: a whole 2x2x4 slice. The times are simulated.
32 devices in a mesh: row: 4 (over z), col: 8 (over y, x, core).
Axes of the slice: x: 2, y: 2, z: 4, core: 2. Of those that a mesh axis runs over, the one named last changes fastest.
Arguments:
- neighbor: int32 [32, 3072, 3072], P(None, 'col', 'row'), may hold values from 0 to 1, as said below
- true_coords: float32 [32, 3, 3072], P(None, None, ('row', 'col')), as said below
- pred_coords: float32 [32, 3, 3072], P(None, None, ('row', 'col')), as said below
- residue_mask: int32 [32, 3072], P(None, ('row', 'col')), may hold values from 0 to 1, as said below
- single: bfloat16 [32, 3072, 384], P(None, ('row', 'col'))
- ln_gain: float32 [384], replicated, may hold values from 0.1 to 1.9
- w_hidden: bfloat16 [384, 128], replicated, may hold values from -0.3125 to 0.3125
- b_hidden: float32 [128], replicated, may hold values from -3 to 3
- w_mid: bfloat16 [128, 128], replicated, may hold values from -0.5 to 0.5
- b_mid: float32 [128], replicated, may hold values from -3 to 3
- w_logits: bfloat16 [128, 50], replicated, may hold values from -1.5 to 1.5
- b_logits: float32 [50], replicated, may hold values from -4 to 4
Outputs:
- lddt_score: float32 [32, 3072], P(None, ('row', 'col'))
- residue_loss: float32 [32, 3072], P(None, ('row', 'col'))
- total_loss: float32 [], replicated
Inputs may be any that keep to these rules, and one draw needn't show every extreme that they name: `neighbor`: 0 or 1; 0 where j == i; 1 wherever 0 < |i - j| <= 8. `residue_mask`: per structure, 1 on a leading run of 1536 or more residues and 0 after it. `true_coords`: positions in angstroms. `pred_coords`: positions in angstroms.
All inputs are finite; a program needn't handle non-finite values.
Results may differ from a plain program's by a relative error of at most 0.00098.
Values sent between devices are 32-bit elements; how exact they have to be, the bound alone decides.
A program may use at most 128 MiB of HBM per device.

v0:
```python
import jax
import jax.numpy as jnp
from jax import lax
from jax.sharding import PartitionSpec as P

L = 3072
THRESHOLDS = (0.5, 1.0, 2.0, 4.0)


def from_root(shard, axis, root):
    mine = lax.axis_index(axis) == root
    return lax.psum(jnp.where(mine, shard, jnp.zeros_like(shard)), axis)


def tile_dist(rows_block, cols_block):
    total = (cols_block[:, 0, :, None] - rows_block[:, 0, None, :]) ** 2
    total = total + (cols_block[:, 1, :, None] - rows_block[:, 1, None, :]) ** 2
    total = total + (cols_block[:, 2, :, None] - rows_block[:, 2, None, :]) ** 2
    return jnp.sqrt(total + 1e-10)


def head_loss(lddt_value, single, ln_gain, w_hidden, b_hidden, w_mid, b_mid, w_logits, b_logits):
    features = single.astype(jnp.float32)
    average = jnp.mean(features, axis=-1, keepdims=True)
    centred = features - average
    variance = jnp.mean(centred * centred, axis=-1, keepdims=True)
    normed = (centred * lax.rsqrt(variance + 1e-05) * ln_gain).astype(jnp.bfloat16)
    first_hidden = jax.nn.relu(
        jnp.dot(normed, w_hidden, preferred_element_type=jnp.float32) + b_hidden
    ).astype(jnp.bfloat16)
    second_hidden = jax.nn.relu(
        jnp.dot(first_hidden, w_mid, preferred_element_type=jnp.float32) + b_mid
    ).astype(jnp.bfloat16)
    logits = jnp.dot(second_hidden, w_logits, preferred_element_type=jnp.float32) + b_logits
    log_total = jnp.log(jnp.sum(jnp.exp(logits), axis=-1))
    bins = logits.shape[-1]
    centers = (jnp.arange(bins).astype(jnp.float32) + 0.5) / bins
    closeness = jnp.exp(-((lddt_value[..., None] - centers) ** 2) * (bins * bins * 0.5))
    target = closeness / jnp.sum(closeness, axis=-1, keepdims=True)
    return log_total - jnp.sum(target * logits, axis=-1)


def local(
    neighbor,
    true_coords,
    pred_coords,
    residue_mask,
    single,
    ln_gain,
    w_hidden,
    b_hidden,
    w_mid,
    b_mid,
    w_logits,
    b_logits,
):
    valid = residue_mask.astype(jnp.float32)
    own_len = residue_mask.shape[1]
    stacked = jnp.concatenate([true_coords, pred_coords, valid[:, None, :]], axis=1)
    row_count = lax.axis_size("row")
    col_count = lax.axis_size("col")
    rows_len = L // row_count
    cols_len = L // col_count
    col_index = lax.axis_index("col")
    rows_part = lax.all_gather(stacked, "col", axis=2, tiled=True)
    offset = col_index * cols_len % rows_len
    column_piece = lax.dynamic_slice_in_dim(rows_part, offset, cols_len, 2)
    source_row = col_index * cols_len // rows_len
    cols_part = from_root(column_piece, "row", source_row)
    true_dist = tile_dist(rows_part[:, 0:3], cols_part[:, 0:3])
    pred_dist = tile_dist(rows_part[:, 3:6], cols_part[:, 3:6])
    mismatch = jnp.abs(pred_dist - true_dist)
    scores = jnp.zeros_like(mismatch)
    for threshold in THRESHOLDS:
        scores = scores + jax.nn.sigmoid(4.0 * (threshold - mismatch))
    scores = 0.25 * scores
    weights = neighbor.astype(jnp.float32) * rows_part[:, 6, None, :] * cols_part[:, 6, :, None]
    preserved = jnp.sum(weights * scores, axis=1)
    neighbors = jnp.sum(weights, axis=1)
    preserved_all, neighbors_all = lax.psum((preserved, neighbors), "col")
    preserved_own = lax.dynamic_slice_in_dim(preserved_all, col_index * own_len, own_len, 1)
    neighbors_own = lax.dynamic_slice_in_dim(neighbors_all, col_index * own_len, own_len, 1)
    lddt_score = preserved_own / jnp.maximum(neighbors_own, 1.0)
    residue_loss = valid * head_loss(
        lddt_score, single, ln_gain, w_hidden, b_hidden, w_mid, b_mid, w_logits, b_logits
    )
    loss_sum, valid_sum = lax.psum((jnp.sum(residue_loss), jnp.sum(valid)), ("row", "col"))
    total_loss = loss_sum / valid_sum
    return (lddt_score, residue_loss, total_loss)


def solution(mesh):
    placed = (
        P(None, "col", "row"),
        P(None, None, ("row", "col")),
        P(None, None, ("row", "col")),
        P(None, ("row", "col")),
        P(None, ("row", "col"), None),
        P(),
        P(),
        P(),
        P(),
        P(),
        P(),
        P(),
    )
    return jax.shard_map(
        local,
        mesh=mesh,
        in_specs=placed,
        out_specs=(P(None, ("row", "col")), P(None, ("row", "col")), P()),
        check_vma=False,
    )
```

profile of v0, /device:TPU:0, one launch (start us, length us, event | category | flops | bytes accessed | tf_op | source)
XLA Modules:
  0.0 312.7 jit_solution(15335422747212448188)
XLA Ops:
  7.3 0.7 convert_bitcast_fusion
  8.0 0.8 pad_maximum_fusion
  8.8 0.9 copy.33
  9.7 21.3 %all_gather.3 = f32[32,7,768]{0,1,2:T(8,128)S(1)} all-gather(f32[32,7,96]{0,1,2:T(8,128)} %copy.33), channel_id=1, replica_groups=mesh['row'=4,'col'=8] {'col'}, dimensions={2}, use_global_device_ids=true | all-gather | bytes 774144 | tf_op jit(solution)/shard_map/all_gather | solution.py:65
  31.0 1.3 dynamic-slice_select_fusion
  32.4 3.3 %fusion.31 = (f32[32,1,768]{0,1,2:T(1,128)}, f32[32,1,768]{0,1,2:T(1,128)}, f32[32,1,768]{0,1,2:T(1,128)}, f32[32,1,768]{0,1,2:T(1,128)}, f32[32,1,768]{0,1,2:T(...) fusion(f32[32,7,768]{0,1,2:T(8,128)S(1)} %all_gather.3), kind=kLoop, calls=%fused_computation.43 | loop fusion | bytes 1376256 | tf_op jit(solution)/shard_map/slice | solution.py:77
  35.6 2.3 convert_reduce_fusion
  37.9 2.8 fusion.4
  40.8 3.2 %maximum_convert_fusion = bf16[32,96,128]{2,1,0:T(8,128)(2,1)S(1)} fusion(bf16[32,96,384]{2,1,0:T(8,128)(2,1)} %param.16, f32[384]{0:T(512)} %param.17, f32[32,96]{1,0:T(8,128)S(1)} %add_rsqrt_fusion, f32[32,96]{1,0:T(8,128)S(1)} %broadcast_multiply_fusion, f32[128]{0:T(128)} %param.21, f32[128]{0:T(128)} %param.19, bf16[384,128]{1,0:T(8,128)(2,1)S(1)} %copy-done, ...), kind=kOutput, calls=%fused_computation.15 | convolution fusion | flops 410910720 | bytes 3303936 | tf_op jit(solution)/shard_map/dot_general | solution.py:32
  44.0 1.1 copy.34
  45.1 1.1 copy.37
  46.2 1.1 copy.39
  47.4 1.1 copy.41
  48.5 1.1 copy.43
  49.7 1.1 copy.45
  50.8 1.1 copy.47
  51.9 1.4 exponential_reduce_fusion
  53.4 48.4 %all-reduce.5.cloned.1.call-done = f32[32,7,384]{0,1,2:T(8,128)} async-done(((f32[32,7,384]{0,1,2:T(8,128)}), f32[32,7,384]{0,1,2:T(8,128)}) %all-reduce.5.cloned.1.call-update) | async-done | bytes 344080 | tf_op jit(solution)/shard_map/psum | solution.py:12
  101.7 6.8 %fusion.32 = (f32[32,1,384]{0,1,2:T(1,128)S(1)}, f32[32,1,384]{0,1,2:T(1,128)S(1)}, f32[32,1,384]{0,1,2:T(1,128)S(1)}, f32[32,1,384]{0,1,2:T(1,128)S(1)}, f32[32...) fusion(f32[32,7,384]{0,1,2:T(8,128)} %all-reduce.5.cloned.1.call-done), kind=kLoop, calls=%fused_computation.44 | loop fusion | bytes 688128 | tf_op jit(solution)/shard_map/slice | solution.py:77
  108.5 0.1 copy.35
  108.6 0.1 copy.36
  108.7 0.1 copy.38
  108.8 0.1 copy.40
  108.9 0.1 copy.42
  109.1 0.1 copy.44
  109.2 0.1 copy.46
  109.3 98.8 %multiply_reduce_fusion = (f32[32,768]{1,0:T(8,128)}, f32[32,768]{1,0:T(8,128)}) fusion(s32[32,384,768]{2,1,0:T(8,128)} %param.12, f32[32,768]{1,0:T(8,128)S(1)} %copy.47, f32[32,384]{1,0:T(8,128)S(1)} %copy.46, f32[32,768]{1,0:T(8,128)S(1)} %copy.45, f32[32,384]{1,0:T(8,128)S(1)} %copy.44, f32[32,768]{1,0:T(8,128)S(1)} %copy.43, f32[32,384]{1,0:T(8,128)S(1)} %copy.42, ...), kind=kLoop, calls=%fused_computation.1 | loop fusion | flops 471810048 | bytes 38977536 | tf_op jit(solution)/shard_map/reduce_sum | solution.py:78
  208.2 53.1 %all-reduce.7.cloned.1.call-done = (f32[32,768]{1,0:T(8,128)}, f32[32,768]{1,0:T(8,128)}) async-done(((f32[32,768]{1,0:T(8,128)}, f32[32,768]{1,0:T(8,128)}), (f32[32,768]{1,0:T(8,128)}, f32[32,768]{1,0:T(8,128)})) %all-reduce.7.cloned.1.call-update) | async-done | bytes 196624 | tf_op jit(solution)/shard_map/psum | solution.py:80
  261.3 0.9 maximum_divide_fusion
  262.1 0.4 fusion.33
  262.6 1.3 fusion.30
  263.9 39.6 %all-reduce = (f32[]{:T(128)}, f32[]{:T(128)}) all-reduce(f32[]{:T(128)} %get-tuple-element.12, f32[]{:T(128)} %get-tuple-element.28), channel_id=1, replica_groups=mesh['row'=4,'col'=8] {'row','col'}, use_global_device_ids=true, to_apply=%region_11.12 | all-reduce | flops 2 | bytes 16 | tf_op jit(solution)/shard_map/psum | solution.py:87
  (13 shorter events, 0.2 us)
Async XLA Ops:
  7.2 33.6 %copy-start = (bf16[384,128]{1,0:T(8,128)(2,1)S(1)}, bf16[384,128]{1,0:T(8,128)(2,1)}, u32[]{:S(2)}) copy-start(bf16[384,128]{1,0:T(8,128)(2,1)} %param.18) | copy-start | bytes 294916
  7.2 94.6 %all-reduce.5.cloned.1.call-start = ((), (), s32[]{:S(2)}) async-start(), calls=%async_computation | async-start | bytes 3145728 | tf_op jit(solution)/shard_map/psum | solution.py:12
  32.3 228.9 %all-reduce.7.cloned.1.call-start = ((), (), s32[]{:S(2)}) async-start(), calls=%async_computation.1 | async-start | bytes 393216 | tf_op jit(solution)/shard_map/psum | solution.py:80
  109.3 153.3 %copy-start.1 = (s32[32,96]{1,0:T(8,128)S(1)}, s32[32,96]{1,0:T(8,128)}, u32[]{:S(2)}) copy-start(s32[32,96]{1,0:T(8,128)} %param.15) | copy-start | bytes 36868
  262.1 42.6 %copy-start.2 = (f32[32,96]{1,0:T(8,128)}, f32[32,96]{1,0:T(8,128)S(1)}, u32[]{:S(2)}) copy-start(f32[32,96]{1,0:T(8,128)S(1)} %maximum_divide_fusion) | copy-start | bytes 36868
Sparse Core Ops, SparseCore 0:
  32.5 69.2 all-reduce.4
  208.3 52.9 all-reduce.6
where the time goes:
time: 314 us; the launch traced here: 313 us
  other arithmetic  109 us (35%)
  waiting for transfers between devices  102 us (32%)
  blocking collectives  60.8 us (19%)
  local copies, waits for them, and re-layouts  19.7 us (6%)
  between operations  16.6 us (5%)
  matrix products  4.59 us (1%)
    reduce_sum x1, other arithmetic, local(): preserved = jnp.sum(weights * scores, axis=1)  98.8 us
    psum x1, waiting for transfers between devices, local(): preserved_all, neighbors_all = lax.psum((preserved, neighbors), 'col')  53.1 us
    psum x1, waiting for transfers between devices, from_root(): return lax.psum(jnp.where(mine, shard, jnp.zeros_like(shard)), axis)  48.4 us
    psum x1, blocking collectives, local(): lax.psum((jnp.sum(residue_loss), jnp.sum(valid)), ('row', 'col'))  39.6 us
    all_gather x1, blocking collectives, local(): rows_part = lax.all_gather(stacked, 'col', axis=2, tiled=True)  21.3 us
    slice x1, local copies, waits for them, and re-layouts, local(): cols_part[:, 6, :, None]  6.78 us
  transfers between devices with their start and end apart: 2, of which 2 were waited for; matrix products, arithmetic and copies ran while one was open for 7% of the time, Pallas kernels for 0%

commit v1 on v0

--- a/solution.py
+++ b/solution.py
@@ -62,7 +62,12 @@
     rows_len = L // row_count
     cols_len = L // col_count
     col_index = lax.axis_index("col")
-    rows_part = lax.all_gather(stacked, "col", axis=2, tiled=True)
+    ring = [stacked]
+    for hop in range(7):
+        ring.append(lax.ppermute(ring[-1], "col", [(dev, (dev + 1) % 8) for dev in range(8)]))
+    rows_part = jnp.roll(
+        jnp.concatenate(ring[::-1], axis=2), (lax.axis_index("col") + 1) * ring[0].shape[2], axis=2
+    )
     offset = col_index * cols_len % rows_len
     column_piece = lax.dynamic_slice_in_dim(rows_part, offset, cols_len, 2)
     source_row = col_index * cols_len // rows_len

time: 314 us -> 291 us (0.927)
  blocking collectives: 60.8 us -> 39.6 us
  local copies, waits for them, and re-layouts: 19.7 us -> 2.06 us
  waiting for transfers between devices: 102 us -> 118 us
    ppermute x0 -> x7, waiting for transfers between devices: none -> 27.7 us  [local(): lax.ppermute(ring[-1], 'col', [(dev, (dev + 1) % 8) for dev in range(8)])]
    all_gather x1 -> x0, blocking collectives: 21.3 us -> none  [local(): rows_part = lax.all_gather(stacked, 'col', axis=2, tiled=True)]
    psum x1, waiting for transfers between devices: 48.4 us -> 36 us  [from_root(): return lax.psum(jnp.where(mine, shard, jnp.zeros_like(shard)), axis)]
    slice x2 -> x0, local copies, waits for them, and re-layouts: 10 us -> none  [the longest x1 6.78 us: local(): cols_part[:, 6, :, None]]
    sub x12 -> x0, local copies, waits for them, and re-layouts: 7.5 us -> none  [the longest x4 2.5 us: tile_dist(): total = total + (cols_block[:, 1, :, None] - rows_block[:, 1, None, :]) ** 2]
  transfers between devices with their start and end apart: 2 -> 9, of which waited for: 2 -> 9; matrix products, arithmetic and copies ran while one was open for 7% -> 3% of each run, Pallas kernels for 0% -> 0%
where the time goes in v1:
time: 291 us; the launch traced here: 290 us
  waiting for transfers between devices  118 us (41%)
  other arithmetic  109 us (37%)
  blocking collectives  39.6 us (14%)
  between operations  16.6 us (6%)
  matrix products  4.58 us (2%)
    reduce_sum x1, other arithmetic, local(): preserved = jnp.sum(weights * scores, axis=1)  98.8 us
    psum x1, waiting for transfers between devices, local(): preserved_all, neighbors_all = lax.psum((preserved, neighbors), 'col')  53.8 us
    psum x1, blocking collectives, local(): lax.psum((jnp.sum(residue_loss), jnp.sum(valid)), ('row', 'col'))  39.6 us
    psum x1, waiting for transfers between devices, from_root(): return lax.psum(jnp.where(mine, shard, jnp.zeros_like(shard)), axis)  36 us
    ppermute x7, waiting for transfers between devices, local(): lax.ppermute(ring[-1], 'col', [(dev, (dev + 1) % 8) for dev in range(8)])  27.7 us
  transfers between devices with their start and end apart: 9, of which 9 were waited for; matrix products, arithmetic and copies ran while one was open for 3% of the time, Pallas kernels for 0%

profile of v1, /device:TPU:0, one launch (start us, length us, event | category | flops | bytes accessed | tf_op | source)
XLA Modules:
  0.0 289.9 jit_solution(3583000818786891710)
XLA Ops:
  7.2 0.0 copy-start
  7.2 0.0 all-reduce.5.cloned.1.call-start
  7.2 0.7 convert_bitcast_fusion
  7.9 0.8 pad_maximum_fusion
  8.8 0.5 collective-permute-start
  9.3 5.3 %collective-permute-done = f32[32,7,96]{2,0,1:T(8,128)S(1)} collective-permute-done((f32[32,7,96]{2,0,1:T(8,128)S(1)}, f32[32,7,96]{2,0,1:T(8,128)S(1)}, u32[]{:S(2)}, u32[]{:S(2)}) %collective-permute-start) | collective-permute-done | bytes 86048 | tf_op jit(solution)/shard_map/ppermute | solution.py:67
  14.7 5.1 %collective-permute-done.1 = f32[32,7,96]{2,0,1:T(8,128)S(1)} collective-permute-done((f32[32,7,96]{2,0,1:T(8,128)S(1)}, f32[32,7,96]{2,0,1:T(8,128)S(1)}, u32[]{:S(2)}, u32[]{:S(2)}) %collective-permute-start.1) | collective-permute-done | bytes 86048 | tf_op jit(solution)/shard_map/ppermute | solution.py:67
  19.8 2.3 convert_reduce_fusion
  22.1 2.8 collective-permute-done.2
  24.9 5.1 %collective-permute-done.3 = f32[32,7,96]{2,0,1:T(8,128)S(1)} collective-permute-done((f32[32,7,96]{2,0,1:T(8,128)S(1)}, f32[32,7,96]{2,0,1:T(8,128)S(1)}, u32[]{:S(2)}, u32[]{:S(2)}) %collective-permute-start.3) | collective-permute-done | bytes 86048 | tf_op jit(solution)/shard_map/ppermute | solution.py:67
  30.0 2.8 fusion.4
  32.8 2.3 collective-permute-done.4
  35.2 5.1 %collective-permute-done.5 = f32[32,7,96]{2,0,1:T(8,128)S(1)} collective-permute-done((f32[32,7,96]{2,0,1:T(8,128)S(1)}, f32[32,7,96]{2,0,1:T(8,128)S(1)}, u32[]{:S(2)}, u32[]{:S(2)}) %collective-permute-start.5) | collective-permute-done | bytes 86048 | tf_op jit(solution)/shard_map/ppermute | solution.py:67
  40.3 3.2 %maximum_convert_fusion = bf16[32,96,128]{2,1,0:T(8,128)(2,1)S(1)} fusion(bf16[32,96,384]{2,1,0:T(8,128)(2,1)} %param.16, f32[384]{0:T(512)} %param.17, f32[32,96]{1,0:T(8,128)S(1)} %add_rsqrt_fusion, f32[32,96]{1,0:T(8,128)S(1)} %broadcast_multiply_fusion, f32[128]{0:T(128)} %param.21, f32[128]{0:T(128)} %param.19, bf16[384,128]{1,0:T(8,128)(2,1)S(1)} %copy-done, ...), kind=kOutput, calls=%fused_computation.15 | convolution fusion | flops 410910720 | bytes 3303936 | tf_op jit(solution)/shard_map/dot_general | solution.py:32
  43.5 1.9 collective-permute-done.6
  45.4 0.8 concatenate.10
  46.2 0.9 dynamic-slice_select_fusion
  47.1 0.0 all-reduce.5.cloned.1.call-update
  47.1 0.0 all-reduce.7.cloned.1.call-start
  47.2 1.4 exponential_reduce_fusion
  48.6 0.3 dynamic-slice_bitcast_fusion.6
  48.9 36.0 %all-reduce.5.cloned.1.call-done = f32[32,7,384]{2,0,1:T(8,128)} async-done(((f32[32,7,384]{2,0,1:T(8,128)}), f32[32,7,384]{2,0,1:T(8,128)}) %all-reduce.5.cloned.1.call-update) | async-done | bytes 344080 | tf_op jit(solution)/shard_map/psum | solution.py:12
  84.9 1.0 slice_bitcast_fusion.6
  85.9 0.0 copy-start.1
  85.9 98.8 %multiply_reduce_fusion = (f32[32,768]{1,0:T(8,128)}, f32[32,768]{1,0:T(8,128)}) fusion(s32[32,384,768]{2,1,0:T(8,128)} %param.12, f32[32,768]{1,0:T(8,128)S(1)} %get-tuple-element.17, f32[32,384]{1,0:T(8,128)S(1)} %get-tuple-element.19, f32[32,768]{1,0:T(8,128)S(1)} %get-tuple-element.12, f32[32,384]{1,0:T(8,128)S(1)} %get-tuple-element.20, ...), kind=kLoop, calls=%fused_computation.1 | loop fusion | flops 471810048 | bytes 38977536 | tf_op jit(solution)/shard_map/reduce_sum | solution.py:83
  184.7 0.0 all-reduce.7.cloned.1.call-update
  184.8 53.8 %all-reduce.7.cloned.1.call-done = (f32[32,768]{1,0:T(8,128)}, f32[32,768]{1,0:T(8,128)}) async-done(((f32[32,768]{1,0:T(8,128)}, f32[32,768]{1,0:T(8,128)}), (f32[32,768]{1,0:T(8,128)}, f32[32,768]{1,0:T(8,128)})) %all-reduce.7.cloned.1.call-update) | async-done | bytes 196624 | tf_op jit(solution)/shard_map/psum | solution.py:85
  238.5 0.9 maximum_divide_fusion
  239.4 0.0 copy-start.2
  239.4 0.4 fusion.31
  239.9 1.3 fusion.30
  241.2 39.6 %all-reduce = (f32[]{:T(128)}, f32[]{:T(128)}) all-reduce(f32[]{:T(128)} %get-tuple-element.9, f32[]{:T(128)} %get-tuple-element.25), channel_id=1, replica_groups=mesh['row'=4,'col'=8] {'row','col'}, use_global_device_ids=true, to_apply=%region_11.12 | all-reduce | flops 2 | bytes 16 | tf_op jit(solution)/shard_map/psum | solution.py:92
  (12 shorter events, 0.0 us)
Async XLA Ops:
  7.2 33.1 %copy-start = (bf16[384,128]{1,0:T(8,128)(2,1)S(1)}, bf16[384,128]{1,0:T(8,128)(2,1)}, u32[]{:S(2)}) copy-start(bf16[384,128]{1,0:T(8,128)(2,1)} %param.18) | copy-start | bytes 294916
  7.2 77.7 %all-reduce.5.cloned.1.call-start = ((), (), s32[]{:S(2)}) async-start(), calls=%async_computation | async-start | bytes 688128 | tf_op jit(solution)/shard_map/psum | solution.py:12
  8.8 5.9 %collective-permute-start = (f32[32,7,96]{2,0,1:T(8,128)S(1)}, f32[32,7,96]{2,0,1:T(8,128)S(1)}, u32[]{:S(2)}, u32[]{:S(2)}) collective-permute-start(f32[32,7,96]{2,0,1:T(8,128)S(1)} %pad_maximum_fusion), channel_id=1, source_target_pairs={{0,1},{1,2},{2,3},{3,4},{4,5},{5,6},{6,7},{7,0},{8,9},{9,10},{10,1... | collective-permute-start | bytes 258056 | tf_op jit(solution)/shard_map/ppermute | solution.py:67
  14.7 5.1 %collective-permute-start.1 = (f32[32,7,96]{2,0,1:T(8,128)S(1)}, f32[32,7,96]{2,0,1:T(8,128)S(1)}, u32[]{:S(2)}, u32[]{:S(2)}) collective-permute-start(f32[32,7,96]{2,0,1:T(8,128)S(1)} %collective-permute-done), channel_id=1, source_target_pairs={{0,1},{1,2},{2,3},{3,4},{4,5},{5,6},{6,7},{7,0},{8,9},{9,10},{10,1... | collective-permute-start | bytes 258056 | tf_op jit(solution)/shard_map/ppermute | solution.py:67
  19.8 5.1 %collective-permute-start.2 = (f32[32,7,96]{2,0,1:T(8,128)S(1)}, f32[32,7,96]{2,0,1:T(8,128)S(1)}, u32[]{:S(2)}, u32[]{:S(2)}) collective-permute-start(f32[32,7,96]{2,0,1:T(8,128)S(1)} %collective-permute-done.1), channel_id=1, source_target_pairs={{0,1},{1,2},{2,3},{3,4},{4,5},{5,6},{6,7},{7,0},{8,9},{9,10},{10,1... | collective-permute-start | bytes 258056 | tf_op jit(solution)/shard_map/ppermute | solution.py:67
  24.9 5.1 %collective-permute-start.3 = (f32[32,7,96]{2,0,1:T(8,128)S(1)}, f32[32,7,96]{2,0,1:T(8,128)S(1)}, u32[]{:S(2)}, u32[]{:S(2)}) collective-permute-start(f32[32,7,96]{2,0,1:T(8,128)S(1)} %collective-permute-done.2), channel_id=1, source_target_pairs={{0,1},{1,2},{2,3},{3,4},{4,5},{5,6},{6,7},{7,0},{8,9},{9,10},{10,1... | collective-permute-start | bytes 258056 | tf_op jit(solution)/shard_map/ppermute | solution.py:67
  30.0 5.1 %collective-permute-start.4 = (f32[32,7,96]{2,0,1:T(8,128)S(1)}, f32[32,7,96]{2,0,1:T(8,128)S(1)}, u32[]{:S(2)}, u32[]{:S(2)}) collective-permute-start(f32[32,7,96]{2,0,1:T(8,128)S(1)} %collective-permute-done.3), channel_id=1, source_target_pairs={{0,1},{1,2},{2,3},{3,4},{4,5},{5,6},{6,7},{7,0},{8,9},{9,10},{10,1... | collective-permute-start | bytes 258056 | tf_op jit(solution)/shard_map/ppermute | solution.py:67
  35.1 5.1 %collective-permute-start.5 = (f32[32,7,96]{2,0,1:T(8,128)S(1)}, f32[32,7,96]{2,0,1:T(8,128)S(1)}, u32[]{:S(2)}, u32[]{:S(2)}) collective-permute-start(f32[32,7,96]{2,0,1:T(8,128)S(1)} %collective-permute-done.4), channel_id=1, source_target_pairs={{0,1},{1,2},{2,3},{3,4},{4,5},{5,6},{6,7},{7,0},{8,9},{9,10},{10,1... | collective-permute-start | bytes 258056 | tf_op jit(solution)/shard_map/ppermute | solution.py:67
  40.3 5.1 %collective-permute-start.6 = (f32[32,7,96]{2,0,1:T(8,128)S(1)}, f32[32,7,96]{2,0,1:T(8,128)S(1)}, u32[]{:S(2)}, u32[]{:S(2)}) collective-permute-start(f32[32,7,96]{2,0,1:T(8,128)S(1)} %collective-permute-done.5), channel_id=1, source_target_pairs={{0,1},{1,2},{2,3},{3,4},{4,5},{5,6},{6,7},{7,0},{8,9},{9,10},{10,1... | collective-permute-start | bytes 258056 | tf_op jit(solution)/shard_map/ppermute | solution.py:67
  47.1 191.4 %all-reduce.7.cloned.1.call-start = ((), (), s32[]{:S(2)}) async-start(), calls=%async_computation.1 | async-start | bytes 393216 | tf_op jit(solution)/shard_map/psum | solution.py:85
  85.9 154.0 %copy-start.1 = (s32[32,96]{1,0:T(8,128)S(1)}, s32[32,96]{1,0:T(8,128)}, u32[]{:S(2)}) copy-start(s32[32,96]{1,0:T(8,128)} %param.15) | copy-start | bytes 36868
  239.4 42.6 %copy-start.2 = (f32[32,96]{1,0:T(8,128)}, f32[32,96]{1,0:T(8,128)S(1)}, u32[]{:S(2)}) copy-start(f32[32,96]{1,0:T(8,128)S(1)} %maximum_divide_fusion) | copy-start | bytes 36868
Sparse Core Ops, SparseCore 0:
  47.2 37.6 all-reduce.4
  184.9 53.6 all-reduce.6
